TPU v7x, 32 devices: a whole 2x2x4 slice. The times are simulated.
32 devices in a mesh: dp: 2 (over x), sp: 16 (over y, z, core).
Axes of the slice: x: 2, y: 2, z: 4, core: 2. Of those that a mesh axis runs over, the one named last changes fastest.
Arguments:
- q: bfloat16 [64, 56, 128], P('dp'), parts along dimension 0
- k: bfloat16 [64, 8192, 8, 128], P('dp', 'sp'), parts along dimension 0
- v: bfloat16 [64, 8192, 8, 128], P('dp', 'sp'), parts along dimension 0
Outputs:
- q: bfloat16 [64, 56, 128], P('dp'), parts along dimension 0
There are 2 independent parts. A program takes and returns all parts, laid end to end along the dimension named above; each array names one.
All inputs are finite; a program needn't handle non-finite values.
Results may differ from a plain program's by a relative error of at most 0.012.
Values are sent between devices in bfloat16 or wider.
A program may use at most 2 GiB of HBM per device.

v0:
```python
import jax
import jax.numpy as jnp
from jax import lax
from jax.sharding import PartitionSpec as P


def einsum(form, a, b):
    return jnp.einsum(form, a.astype(jnp.float32), b.astype(jnp.float32))


def part_of(q, k, v):
    grouped = q.reshape(q.shape[0], k.shape[2], -1, q.shape[2])
    scores = einsum("bgsd,bugd->bgsu", grouped, k) * q.shape[2] ** -0.5
    high = jnp.max(scores, -1, keepdims=True)
    weights = jnp.exp(scores - high)
    seen = einsum("bgsu,bugd->bgsd", weights.astype(jnp.bfloat16), v)
    return jnp.concatenate([seen, jnp.sum(weights, -1, keepdims=True), high], -1)


def together(parts):
    seen, total, high = parts[..., :-2], parts[..., -2:-1], parts[..., -1:]
    scale = jnp.exp(high - jnp.max(high, 0))
    return (jnp.sum(seen * scale, 0) / jnp.sum(total * scale, 0)).astype(jnp.bfloat16)


def solution(mesh):
    def step(q, k, v):
        return together(lax.all_gather(part_of(q, k, v), "sp")).reshape(q.shape)

    return jax.shard_map(
        step,
        mesh=mesh,
        in_specs=(P("dp", None, None), P("dp", "sp", None, None), P("dp", "sp", None, None)),
        out_specs=P("dp", None, None),
        check_vma=False,
    )
```

profile of v0, /device:TPU:0, one launch (start us, length us, event | category | flops | bytes accessed | tf_op | source)
XLA Modules:
  0.0 253.7 jit_solution(7656546816402922171)
XLA Ops:
  6.5 0.0 all-gather.3.cloned.1.call-start
  6.5 1.1 copy.46
  7.6 14.4 %multiply_reduce_fusion = (f32[32,8,7]{2,1,0:T(8,128)S(1)}, f32[32,8,7,512]{3,2,1,0:T(8,128)S(1)}) fusion(bf16[32,512,8,128]{3,2,1,0:T(8,128)(2,1)} %param.4, bf16[32,8,7,128]{3,0,2,1:T(8,128)(2,1)S(1)} %bitcast.14), kind=kOutput, calls=%fused_computation.7 | convolution fusion | flops 236714240 | bytes 37690368 | tf_op jit(solution)/shard_map/bgsd,bugd->bgsu/dot_general | solution.py:8
  22.0 0.0 copy-start
  22.0 1.9 copy-done
  24.0 1.2 fusion.5
  25.1 16.2 %fusion = f32[32,8,7,128]{3,2,1,0:T(8,128)S(1)} fusion(bf16[32,512,8,128]{3,2,1,0:T(8,128)(2,1)} %param.5, f32[32,8,7,512]{3,2,1,0:T(8,128)} %copy-done, f32[32,8,7]{2,1,0:T(8,128)S(1)} %get-tuple-element.10), kind=kOutput, calls=%fused_computation | convolution fusion | flops 237633536 | bytes 38149120 | tf_op jit(solution)/shard_map/bgsu,bugd->bgsd/dot_general | solution.py:8
  41.4 1.7 copy.52
  43.1 1.7 copy.53
  44.7 0.4 pad_maximum_fusion
  45.1 2.0 copy.54
  47.2 0.0 all-gather.3.cloned.1.call-update
  47.2 151.1 %all-gather.3.cloned.1.call-done = f32[512,8,7,130]{3,1,2,0:T(8,128)} async-done(((f32[32,8,7,130]{3,1,2,0:T(8,128)}), f32[512,8,7,130]{3,1,2,0:T(8,128)}) %all-gather.3.cloned.1.call-update) | async-done | bytes 14909456 | tf_op jit(solution)/shard_map/all_gather | solution.py:28
  198.3 19.7 %fusion.14 = (f32[16,32,8,7,1]{4,2,3,1,0:T(8,128)}, f32[32,8,7]{1,2,0:T(8,128)S(1)}, f32[16,32,8,7,1]{4,2,3,1,0:T(8,128)}) fusion(f32[16,32,8,7,130]{4,2,3,1,0:T(8,128)} %bitcast.12), kind=kLoop, calls=%fused_computation.21 | loop fusion | flops 26880 | bytes 465920 | tf_op jit(solution)/shard_map/slice | solution.py:21
  218.0 9.6 %copy.68 = f32[16,32,8,7,1]{1,2,4,3,0:T(8,128)S(1)} copy(f32[16,32,8,7,1]{4,2,3,1,0:T(8,128)} %get-tuple-element.5) | data formatting | bytes 229376
  227.6 0.1 copy.70
  227.7 9.6 %copy.67 = f32[16,32,8,7,1]{1,2,4,3,0:T(8,128)S(1)} copy(f32[16,32,8,7,1]{4,2,3,1,0:T(8,128)} %get-tuple-element.7) | data formatting | bytes 229376
  237.4 0.1 multiply_reduce_fusion.1
  237.5 0.7 copy.56
  238.2 7.2 %fusion.4 = f32[32,8,7,128]{3,1,2,0:T(8,128)S(1)} fusion(f32[16,32,8,7,130]{4,2,3,1,0:T(8,128)} %bitcast.13, f32[16,32,8,7]{2,3,1,0:T(8,128)S(1)} %copy.56), kind=kLoop, calls=%fused_computation.5 | loop fusion | flops 7110656 | bytes 15712256 | tf_op jit(solution)/shard_map/reduce_sum | solution.py:23
  245.4 0.2 copy.58
  245.6 0.3 fusion.10
  245.9 0.9 copy.61
  (2 shorter events, 0.0 us)
Async XLA Ops:
  6.5 191.7 %all-gather.3.cloned.1.call-start = ((), (), s32[]{:S(2)}) async-start(), calls=%async_computation | async-start | bytes 31195136 | tf_op jit(solution)/shard_map/all_gather | solution.py:28
  22.0 1.9 copy-start
Sparse Core Ops, SparseCore 0:
  47.3 150.9 all-gather.2
where the time goes:
time: 254 us
  waiting for transfers between devices  151 us (59%)
  matrix products  30.6 us (12%)
  local copies, waits for them, and re-layouts  29.6 us (12%)
  other arithmetic  28.9 us (11%)
  between operations  13.5 us (5%)
    all_gather x1, waiting for transfers between devices, step(): return together(lax.all_gather(part_of(q, k, v), 'sp')).reshape(q.shape)  151 us
    dot_general x2, matrix products, einsum(): return jnp.einsum(form, a.astype(jnp.float32), b.astype(jnp.float32))  30.6 us
    unnamed x6, local copies, waits for them, and re-layouts  22.4 us
    slice x1, other arithmetic, together(): seen, total, high = (parts[..., :-2], parts[..., -2:-1], parts[..., -1:])  19.7 us
    reduce_sum x1, other arithmetic, together(): jnp.sum(seen * scale, 0) / jnp.sum(total * scale, 0)  7.16 us
  transfers between devices with their start and end apart: 1, of which 1 were waited for; matrix products, arithmetic and copies ran while one was open for 0% of the time, Pallas kernels for 0%

commit v1 on v0

v1 whole, which is shorter than its diff:
```python
import math

import jax
import jax.numpy as jnp
from jax import lax
from jax.experimental import pallas as pl
from jax.experimental.pallas import tpu as pltpu
from jax.sharding import PartitionSpec as P

MESH = pl.DeviceIdType.MESH
SLOTS = 6
LAG = 5
G = 8
W = 256


def kernel(q_ref, k_ref, v_ref, o_ref, kbuf, vbuf, qbuf, qq, bias, sbuf, hbuf, ksem, vsem, qsem,
           near_out, near_out_st, near_in, near_in_st, mine, mine_st, far_out, far_out_st, far_in, far_in_st, owned, owned_st, done,
           near_send, near_recv, far_send, far_recv, all_send, all_recv, done_sem):
    B, H, D = q_ref.shape
    S = H // G
    half = k_ref.shape[1] // 2
    NC = half // W
    T = H // 8
    pairs = B // 2
    c = D ** -0.5 * math.log2(math.e)
    me = lax.axis_index("sp")
    n = lax.axis_size("sp")
    chips = n // 2
    core = lax.rem(me, 2)
    chip = me // 2

    def seq(j, u):
        return 2 * j + core if u else 2 * j + 1 - core

    def owner(j):
        r = lax.rem(j, chips)
        x = lax.rem(3 + 2 * (r // 2), 5)
        z = x - 3 * (x // 4)
        z = z + core * (3 - 2 * z)
        return lax.rem(r + core, 2) * 4 + z

    def kcopy(j, u):
        s = lax.rem(2 * j + u, SLOTS)
        return pltpu.make_async_copy(k_ref.at[seq(j, u)], kbuf.at[s], ksem.at[s])

    def vcopy(j, u):
        s = lax.rem(2 * j + u, SLOTS)
        return pltpu.make_async_copy(v_ref.at[seq(j, u)], vbuf.at[s], vsem.at[s])

    def near(j):
        to = {"sp": me + 1 - 2 * core}
        return [
            pltpu.make_async_remote_copy(near_out.at[j], near_in.at[j], near_send.at[0, j], near_recv.at[0, j], device_id=to, device_id_type=MESH),
            pltpu.make_async_remote_copy(near_out_st.at[j], near_in_st.at[j], near_send.at[1, j], near_recv.at[1, j], device_id=to, device_id_type=MESH),
        ]

    def far(j, at, to):
        s = j // chips
        to = {"sp": 2 * to + core}
        return [
            pltpu.make_async_remote_copy(far_out.at[j], far_in.at[s, at], far_send.at[0, j], far_recv.at[0, s, at], device_id=to, device_id_type=MESH),
            pltpu.make_async_remote_copy(far_out_st.at[j], far_in_st.at[s, at], far_send.at[1, j], far_recv.at[1, s, at], device_id=to, device_id_type=MESH),
        ]

    def spread(j, i, b):
        return pltpu.make_async_remote_copy(done.at[j // chips], o_ref.at[b], all_send.at[j // chips, i], all_recv.at[b],
                                            device_id={"sp": lax.rem(me + i, n)}, device_id_type=MESH)

    def kept(j, b):
        return pltpu.make_async_copy(done.at[j // chips], o_ref.at[b], done_sem.at[j // chips])

    barrier = pltpu.get_barrier_semaphore()
    for i in range(1, n):
        pl.semaphore_signal(barrier, inc=1, device_id={"sp": lax.rem(me + i, n)}, device_id_type=MESH)
    qc = pltpu.make_async_copy(q_ref, qbuf, qsem)
    qc.start()
    held = SLOTS // 2
    for j in range(held + 1):
        for u in range(2):
            if j < held:
                kcopy(j, u).start()
            if j >= 1:
                vcopy(j - 1, u).start()
    row = lax.broadcasted_iota(jnp.int32, (H, W), 0)
    col = lax.broadcasted_iota(jnp.int32, (H, W), 1)
    bias[...] = jnp.where(row // S == lax.rem(col, G), jnp.inf, -jnp.inf)
    lane = lax.broadcasted_iota(jnp.int32, (8, 128), 1)
    qc.wait()

    def prep(b, _):
        x = qbuf[b].astype(jnp.float32)
        z = jnp.zeros_like(x)
        qq[b] = jnp.concatenate([jnp.concatenate([x, z], 1), jnp.concatenate([z, x], 1)], 0).astype(jnp.bfloat16)
        return 0
    lax.fori_loop(0, B, prep, 0)

    def side(buf, slot, i):
        return jnp.concatenate([buf[slot, i * W:(i + 1) * W], buf[slot, half + i * W:half + (i + 1) * W]], 1)

    def attend(jv, jk, us, outs):
        bb = bias[...]
        bb = jnp.concatenate([bb, bb], 0)
        if jv is not None:
            highs = {u: jnp.max(hbuf[u], 1, keepdims=True) for u in us}
        for u in us:
            high = total = acc = None
            if jv is not None:
                high2 = jnp.concatenate([highs[u], highs[u]], 0)
                vslot = lax.rem(2 * jv + u, SLOTS)
            if jk is not None:
                lhs = qq[seq(jk, u)]
                kslot = lax.rem(2 * jk + u, SLOTS)
            for i in range(NC):
                if jv is not None:
                    p = jnp.exp2((sbuf[u, i] - high2) * c)
                    h = p[:, :128] + p[:, 128:]
                    total = h if total is None else total + h
                    a = lax.dot_general(p.astype(jnp.bfloat16), side(vbuf, vslot, i), (((1,), (0,)), ((), ())), preferred_element_type=jnp.float32)
                    acc = a if acc is None else acc + a
                if jk is not None:
                    s = lax.dot_general(lhs, side(kbuf, kslot, i), (((1,), (1,)), ((), ())), preferred_element_type=jnp.float32)
                    s = jnp.minimum(s, bb)
                    sbuf[u, i] = s
                    h = jnp.maximum(s[:, :128], s[:, 128:])
                    h = jnp.maximum(h[:H], h[H:])
                    high = h if high is None else jnp.maximum(high, h)
            if jk is not None:
                hbuf[u] = high
            if jv is not None:
                total = jnp.sum(total[:H] + total[H:], 1, keepdims=True)
                outs(u, acc[:H, :D] + acc[H:, D:], stats(highs[u], total))

    def stats(high, total):
        st = jnp.zeros((8, 128), jnp.float32)
        for t in range(T):
            st = jnp.where(lane == t, high[8 * t:8 * t + 8], st)
            st = jnp.where(lane == 64 + t, total[8 * t:8 * t + 8], st)
        return st

    def scaled(acc, w):
        return [acc[8 * t:8 * t + 8] * w[:, t:t + 1] for t in range(T)]

    def merge(parts):
        high = parts[0]
        for st in parts[1:]:
            high = jnp.maximum(high, st)
        ws = [jnp.exp2((st - high) * c) for st in parts]
        total = None
        for st, w in zip(parts, ws):
            x = w * pltpu.roll(st, 64, 1)
            total = x if total is None else total + x
        return ws, high, total

    def outs(j):
        def f(u, acc, st):
            if u == 0:
                near_out[j] = acc.astype(jnp.bfloat16)
                near_out_st[j] = st
                for x in near(j):
                    x.start()
            else:
                mine[lax.rem(j, 2)] = acc
                mine_st[lax.rem(j, 2)] = st
        return f

    def join(j):
        for x in near(j):
            x.wait_recv()
        sa, sb = mine_st[lax.rem(j, 2)], near_in_st[j]
        (wa, wb), high, total = merge([sa, sb])
        st = jnp.where(lane < 64, high, pltpu.roll(total, 64, 1))
        xa = scaled(mine[lax.rem(j, 2)], wa)
        xb = scaled(near_in[j].astype(jnp.float32), wb)
        acc = jnp.concatenate([x + y for x, y in zip(xa, xb)], 0)
        to = owner(j)

        @pl.when(to == chip)
        def _():
            owned[j // chips] = acc
            owned_st[j // chips] = st

        @pl.when(to != chip)
        def _():
            far_out[j] = acc.astype(jnp.bfloat16)
            far_out_st[j] = st
            for x in far(j, chip, to):
                x.start()

    def finish(j):
        @pl.when(owner(j) == chip)
        def _():
            s = j // chips
            b = seq(j, 1)
            others = [lax.rem(chip + i, chips) for i in range(1, chips)]
            for x in others:
                for y in far(j, x, chip):
                    y.wait_recv()
            ws, _, total = merge([owned_st[s]] + [far_in_st[s, x] for x in others])
            inverse = 1.0 / total
            rows = scaled(owned[s], ws[0] * inverse)
            for x, w in zip(others, ws[1:]):
                rows = [y + z for y, z in zip(rows, scaled(far_in[s, x].astype(jnp.float32), w * inverse))]
            done[s] = jnp.concatenate(rows, 0).astype(jnp.bfloat16)
            for i in range(1, n):
                spread(j, i, b).start()
            kept(j, b).start()

    for u in range(2):
        kcopy(0, u).wait()
    attend(None, 0, (0, 1), None)
    for u in range(2):
        kcopy(held, u).start()
    pl.semaphore_wait(barrier, n - 1)

    def step(j, _):
        for u in range(2):
            vcopy(j, u).wait()
            kcopy(j + 1, u).wait()
        attend(j, j + 1, (0, 1), outs(j))
        for u in range(2):
            @pl.when(j + held < pairs)
            def _():
                vcopy(j + held, u).start()

            @pl.when(j + 1 + held < pairs)
            def _():
                kcopy(j + 1 + held, u).start()

        @pl.when(j >= 1)
        def _():
            join(j - 1)

        @pl.when(j >= LAG)
        def _():
            finish(j - LAG)
        return 0

    lax.fori_loop(0, pairs - 1, step, 0)
    last = pairs - 1
    for u in range(2):
        vcopy(last, u).wait()
        attend(last, None, (u,), outs(last))
    join(last - 1)
    join(last)
    lax.fori_loop(last - LAG, pairs, lambda j, _: (finish(j), 0)[1], 0)

    def drain(j, _):
        for x in near(j):
            x.wait_send()

        @pl.when(owner(j) != chip)
        def _():
            for x in far(j, chip, owner(j)):
                x.wait_send()

        @pl.when(owner(j) == chip)
        def _():
            b = seq(j, 1)
            for i in range(1, n):
                spread(j, i, b).wait_send()
            kept(j, b).wait()
        return 0
    lax.fori_loop(0, pairs, drain, 0)

    def arrive(j, _):
        spread(j, 1, seq(j, 0)).wait_recv()

        @pl.when(owner(j) != chip)
        def _():
            spread(j, 1, seq(j, 1)).wait_recv()
        return 0
    lax.fori_loop(0, pairs, arrive, 0)


def solution(mesh):
    n = mesh.shape["sp"]

    def step(q, k, v):
        B, L, _, D = k.shape
        H = q.shape[1]
        rows = L * G
        pairs = B // 2
        chips = n // 2
        own = pairs // chips
        f32, bf16, vmem, dma = jnp.float32, jnp.bfloat16, pltpu.VMEM, pltpu.SemaphoreType.DMA
        return pl.pallas_call(
            kernel,
            out_shape=jax.ShapeDtypeStruct(q.shape, q.dtype),
            in_specs=[pl.BlockSpec(memory_space=pl.ANY)] * 3,
            out_specs=pl.BlockSpec(memory_space=pl.ANY),
            scratch_shapes=[
                vmem((SLOTS, rows, D), bf16), vmem((SLOTS, rows, D), bf16), vmem((B, H, D), bf16), vmem((B, 2 * H, 2 * D), bf16),
                vmem((H, W), f32), vmem((2, rows // (2 * W), 2 * H, W), f32), vmem((2, H, 128), f32),
                dma((SLOTS,)), dma((SLOTS,)), dma,
                vmem((pairs, H, D), bf16), vmem((pairs, 8, 128), f32), vmem((pairs, H, D), bf16), vmem((pairs, 8, 128), f32),
                vmem((2, H, D), f32), vmem((2, 8, 128), f32),
                vmem((pairs, H, D), bf16), vmem((pairs, 8, 128), f32),
                vmem((own, chips, H, D), bf16), vmem((own, chips, 8, 128), f32),
                vmem((own, H, D), f32), vmem((own, 8, 128), f32), vmem((own, H, D), bf16),
                dma((2, pairs)), dma((2, pairs)), dma((2, pairs)), dma((2, own, chips)), dma((own, n)), dma((B,)), dma((own,)),
            ],
            compiler_params=pltpu.CompilerParams(vmem_limit_bytes=58 << 20, collective_id=0, has_side_effects=True),
            name="attend",
        )(q, k.reshape(B, rows, D), v.reshape(B, rows, D))

    return jax.shard_map(
        step,
        mesh=mesh,
        in_specs=(P("dp", None, None), P("dp", "sp", None, None), P("dp", "sp", None, None)),
        out_specs=P("dp", None, None),
        check_vma=False,
    )
```

time: 254 us -> 49.1 us (0.19)
  waiting for transfers between devices: 151 us -> 0 us
  Pallas kernels: 0 us -> 47.2 us
  matrix products: 30.6 us -> 0 us
  other arithmetic: 28.9 us -> 0 us
  local copies, waits for them, and re-layouts: 29.6 us -> 1.82 us
  between operations: 13.5 us -> 0.01 us
    all_gather x1 -> x0, waiting for transfers between devices: 151 us -> none  [step(): return together(lax.all_gather(part_of(q, k, v), 'sp')).reshape(q.shape)]
    pallas_call x0 -> x1, Pallas kernels: none -> 47.2 us  [step(): pl.pallas_call(kernel, out_shape=jax.ShapeDtypeStruct(q.shape, q.dtype),...]
    dot_general x2 -> x0, matrix products: 30.6 us -> none  [einsum(): return jnp.einsum(form, a.astype(jnp.float32), b.astype(jnp.float32))]
    unnamed x6 -> x1, local copies, waits for them, and re-layouts: 22.4 us -> 1.82 us
    slice x1 -> x0, other arithmetic: 19.7 us -> none  [together(): seen, total, high = (parts[..., :-2], parts[..., -2:-1], parts[..., -1:])]
    reduce_sum x3 -> x0, other arithmetic: 8.43 us -> none  [the longest x1 7.16 us: together(): jnp.sum(seen * scale, 0) / jnp.sum(total * scale, 0)]
    broadcast_in_dim x2 -> x0, local copies, waits for them, and re-layouts: 3.33 us -> none  [the longest x1 1.66 us: part_of(): jnp.sum(weights, -1, keepdims=True)]
  transfers between devices with their start and end apart: 1 -> 0, of which waited for: 1 -> 0; matrix products, arithmetic and copies ran while one was open for 0% -> 0% of each run, Pallas kernels for 0% -> 0%
where the time goes in v1:
time: 49.1 us; the launch traced here: 49 us
  Pallas kernels  47.2 us (96%)
  local copies, waits for them, and re-layouts  1.82 us (4%)
    pallas_call x1, Pallas kernels, step(): pl.pallas_call(kernel, out_shape=jax.ShapeDtypeStruct(q.shape, q.dtype),...  47.2 us
    unnamed x1, local copies, waits for them, and re-layouts  1.82 us

profile of v1, /device:TPU:0, one launch (start us, length us, event | category | flops | bytes accessed | tf_op | source)
XLA Modules:
  0.0 49.0 jit_solution(7837461099472435359)
XLA Ops:
  0.0 47.2 %attend.1 = bf16[32,56,128]{2,1,0:T(8,128)(2,1)} custom-call(bf16[32,56,128]{2,1,0:T(8,128)(2,1)} %q_ref.1, bf16[32,4096,128]{2,1,0:T(8,128)(2,1)} %bitcast.2, bf16[32,4096,128]{2,1,0:T(8,128)(2,1)} %bitcast.3), custom_call_target="tpu_custom_call" | custom-call | tf_op jit(solution)/shard_map/attend/pallas_call | solution.py:287
  47.2 1.8 %copy.5 = bf16[32,56,128]{2,1,0:T(8,128)(2,1)} copy(bf16[32,56,128]{2,1,0:T(8,128)(2,1)} %attend.1) | data formatting | bytes 917504

commit v2 on v1

v2 whole, which is shorter than its diff:
```python
import functools
import math

import jax
import jax.numpy as jnp
from jax import lax
from jax.experimental import pallas as pl
from jax.experimental.pallas import tpu as pltpu
from jax.sharding import PartitionSpec as P

MESH = pl.DeviceIdType.MESH
SLOTS = 8
AHEAD = 3
LAG = 7
HAND = 6
G = 8
W = 256


def kernel(q_ref, k_ref, v_ref, o_ref, kbuf, vbuf, qbuf, qq, bias, sbuf, pbuf, hbuf, mbuf, tbuf, ksem, vsem, qsem,
           near_out, near_out_st, near_in, near_in_st, mine, mine_st, far_out, far_out_st, far_in, far_in_st, done,
           near_send, near_recv, far_send, far_recv, all_send, all_recv):
    B, H, D = q_ref.shape
    S = H // G
    half = k_ref.shape[1] // 2
    NC = half // W
    T = H // 8
    pairs = B // 2
    c = D ** -0.5 * math.log2(math.e)
    me = lax.axis_index("sp")
    n = lax.axis_size("sp")
    chips = n // 2
    core = me & 1
    chip = me >> 1

    def seq(j, u):
        return 2 * j + core if u else 2 * j + 1 - core

    def owner(j):
        low, high = (j >> 1) & 1, (j >> 2) & 1
        z = (2 * (1 ^ low) + (1 ^ low ^ high)) ^ (3 * core)
        return 4 * ((j ^ core) & 1) + z

    def slot(j, u):
        return (2 * j + u) & (SLOTS - 1)

    def kcopy(j, u):
        s = slot(j, u)
        return pltpu.make_async_copy(k_ref.at[seq(j, u)], kbuf.at[s], ksem.at[s])

    def vcopy(j, u):
        s = slot(j, u)
        return pltpu.make_async_copy(v_ref.at[seq(j, u)], vbuf.at[s], vsem.at[s])

    def near(j):
        to = {"sp": me + 1 - 2 * core}
        return [
            pltpu.make_async_remote_copy(near_out.at[j], near_in.at[j], near_send.at[0, j], near_recv.at[0, j], device_id=to, device_id_type=MESH),
            pltpu.make_async_remote_copy(near_out_st.at[j], near_in_st.at[j], near_send.at[1, j], near_recv.at[1, j], device_id=to, device_id_type=MESH),
        ]

    def far(j, at, to):
        s = j >> 3
        to = {"sp": 2 * to + core}
        return [
            pltpu.make_async_remote_copy(far_out.at[j], far_in.at[s, at], far_send.at[0, j], far_recv.at[0, s, at], device_id=to, device_id_type=MESH),
            pltpu.make_async_remote_copy(far_out_st.at[j], far_in_st.at[s, at], far_send.at[1, j], far_recv.at[1, s, at], device_id=to, device_id_type=MESH),
        ]

    def spread(j, b, slot, chip_, core_):
        i = 2 * chip_ + core_
        return pltpu.make_async_remote_copy(done.at[j >> 3], o_ref.at[b], all_send.at[slot, j], all_recv.at[b],
                                            device_id={"sp": i}, device_id_type=MESH)

    def spreads(j, b):
        y, z = chip >> 2, chip & 3
        to = [(((y + dy) & 1) * 4 + ((z + dz) & 3), core) for dy, dz in ((1, 2), (0, 2), (1, 1), (1, 3), (0, 1), (0, 3), (1, 0))]
        return [spread(j, b, i, *x) for i, x in enumerate(to + [(chip, 1 - core)])]

    def forward(b, j):
        return pltpu.make_async_remote_copy(o_ref.at[b], o_ref.at[b], all_send.at[0, j], all_recv.at[b],
                                            device_id={"sp": me + 1 - 2 * core}, device_id_type=MESH)

    barrier = pltpu.get_barrier_semaphore()
    for i in range(1, n):
        pl.semaphore_signal(barrier, inc=1, device_id={"sp": lax.rem(me + i, n)}, device_id_type=MESH)
    qc = pltpu.make_async_copy(q_ref, qbuf, qsem)
    qc.start()
    held = AHEAD

    def fetch(copy, j):
        for u in range(2):
            copy(j, u).start(priority=1)

    def await_(copy, j):
        for u in range(2):
            copy(j, u).wait()

    fetch(kcopy, 0)
    fetch(kcopy, 1)
    fetch(vcopy, 0)
    row = lax.broadcasted_iota(jnp.int32, (H, W), 0)
    col = lax.broadcasted_iota(jnp.int32, (H, W), 1)
    bias[...] = jnp.where(row // S == lax.rem(col, G), jnp.inf, -jnp.inf)
    lane = lax.broadcasted_iota(jnp.int32, (8, 128), 1)
    qc.wait()

    def prep(b, _):
        x = qbuf[b].astype(jnp.float32)
        z = jnp.zeros_like(x)
        qq[b] = jnp.concatenate([jnp.concatenate([x, z], 1), jnp.concatenate([z, x], 1)], 0).astype(jnp.bfloat16)
        return 0
    lax.fori_loop(0, B, prep, 0)

    def side(buf, slot, i):
        return jnp.concatenate([buf[slot, i * W:(i + 1) * W], buf[slot, half + i * W:half + (i + 1) * W]], 1)

    def attend(jv, je, jk, us, outs):
        if jv is not None:
            totals = {u: jnp.sum(tbuf[u], 1, keepdims=True) for u in us}
            for u in us:
                vslot = slot(jv, u)
                acc = None
                for i in range(NC):
                    a = lax.dot_general(pbuf[u, i], side(vbuf, vslot, i), (((1,), (0,)), ((), ())), preferred_element_type=jnp.float32)
                    acc = a if acc is None else acc + a
                outs(u, acc[:H, :D] + acc[H:, D:], stats(mbuf[u], totals[u]))
        if je is not None:
            for u in us:
                high = jnp.broadcast_to(jnp.max(hbuf[u], 1, keepdims=True), (H, 128))
                mbuf[u] = high
                high = jnp.concatenate([jnp.concatenate([high, high], 1)] * 2, 0)
                total = None
                for i in range(NC):
                    p = jnp.exp2((sbuf[u, i] - high) * c)
                    pbuf[u, i] = p.astype(jnp.bfloat16)
                    h = p[:, :128] + p[:, 128:]
                    h = h[:H] + h[H:]
                    total = h if total is None else total + h
                tbuf[u] = total
        if jk is not None:
            bb = bias[...]
            bb = jnp.concatenate([bb, bb], 0)
            for u in us:
                lhs = qq[seq(jk, u)]
                kslot = slot(jk, u)
                high = None
                for i in range(NC):
                    x = lax.dot_general(lhs, side(kbuf, kslot, i), (((1,), (1,)), ((), ())), preferred_element_type=jnp.float32)
                    x = jnp.minimum(x, bb)
                    sbuf[u, i] = x
                    h = jnp.maximum(x[:, :128], x[:, 128:])
                    h = jnp.maximum(h[:H], h[H:])
                    high = h if high is None else jnp.maximum(high, h)
                hbuf[u] = high

    def stats(high, total):
        st = jnp.zeros((8, 128), jnp.float32)
        for t in range(T):
            st = jnp.where(lane == t, high[8 * t:8 * t + 8], st)
            st = jnp.where(lane == 64 + t, total[8 * t:8 * t + 8], st)
        return st

    def scaled(acc, w):
        return [acc[8 * t:8 * t + 8] * w[:, t:t + 1] for t in range(T)]

    def merge(parts):
        high = parts[0]
        for st in parts[1:]:
            high = jnp.maximum(high, st)
        ws = [jnp.exp2((st - high) * c) for st in parts]
        total = None
        for st, w in zip(parts, ws):
            x = w * pltpu.roll(st, 64, 1)
            total = x if total is None else total + x
        return ws, high, total

    def outs(j):
        def f(u, acc, st):
            if u == 0:
                near_out[j] = acc.astype(jnp.bfloat16)
                near_out_st[j] = st
            else:
                mine[j] = acc
                mine_st[j] = st
        return f

    def join(j):
        (wa, wb), high, total = merge([mine_st[j], near_in_st[j]])
        st = jnp.where(lane < 64, high, pltpu.roll(total, 64, 1))
        xa = scaled(mine[j], wa)
        xb = scaled(near_in[j].astype(jnp.float32), wb)
        acc = jnp.concatenate([x + y for x, y in zip(xa, xb)], 0)
        mine[j] = acc
        mine_st[j] = st
        far_out[j] = acc.astype(jnp.bfloat16)
        far_out_st[j] = st

    def near_wait(j):
        for x in near(j):
            x.wait_recv()

    def near_start(j):
        for x in near(j):
            x.start()

    def far_start(j):
        to = owner(j)

        @pl.when(to != chip)
        def _():
            for x in far(j, chip, to):
                x.start()

    def finish(j):
        @pl.when(owner(j) == chip)
        def _():
            s = j >> 3
            b = seq(j, 1)
            others = [(chip + i) & (chips - 1) for i in range(1, chips)]
            for x in others:
                for y in far(j, x, chip):
                    y.wait_recv()
            ws, _, total = merge([mine_st[j]] + [far_in_st[s, x] for x in others])
            inverse = 1.0 / total
            rows = scaled(mine[j], ws[0] * inverse)
            for x, w in zip(others, ws[1:]):
                rows = [y + z for y, z in zip(rows, scaled(far_in[s, x].astype(jnp.float32), w * inverse))]
            done[s] = jnp.concatenate(rows, 0).astype(jnp.bfloat16)
            for x in spreads(j, b):
                x.start()
            o_ref[b] = done[s]

    def hand(j):
        @pl.when(owner(j) != chip)
        def _():
            b = seq(j, 1)
            forward(b, j).wait_recv()
            forward(b, j).start()

    both = (0, 1)
    await_(kcopy, 0)
    fetch(kcopy, 2)
    fetch(vcopy, 1)
    attend(None, None, 0, both, None)
    fetch(kcopy, 3)
    await_(kcopy, 1)
    attend(None, 0, 1, both, None)
    fetch(vcopy, 2)
    fetch(kcopy, 4)

    def step(joins, j, _):
        await_(vcopy, j)
        await_(kcopy, j + 2)
        if joins:
            near_wait(j - 2)
            join(j - 2)
        attend(j, j + 1, j + 2, both, outs(j))
        if not joins:
            @pl.when(j == 0)
            def _():
                pl.semaphore_wait(barrier, n - 1)
        near_start(j)
        if joins:
            far_start(j - 2)

        @pl.when(j + held < pairs)
        def _():
            fetch(vcopy, j + held)

        @pl.when(j + 2 + held < pairs)
        def _():
            fetch(kcopy, j + 2 + held)
        if joins:
            @pl.when(j >= LAG)
            def _():
                finish(j - LAG)

            @pl.when(j >= LAG + HAND)
            def _():
                hand(j - LAG - HAND)
        return 0

    last = pairs - 1
    lax.fori_loop(0, 2, functools.partial(step, False), 0)
    lax.fori_loop(2, last - 1, functools.partial(step, True), 0)
    await_(vcopy, last - 1)
    near_wait(last - 3)
    join(last - 3)
    attend(last - 1, last, None, both, outs(last - 1))
    near_start(last - 1)
    far_start(last - 3)
    near_wait(last - 2)
    join(last - 2)
    far_start(last - 2)
    vcopy(last, 0).wait()
    attend(last, None, None, (0,), outs(last))
    near_start(last)
    finish(last - 1 - LAG)
    near_wait(last - 1)
    join(last - 1)
    far_start(last - 1)
    vcopy(last, 1).wait()
    attend(last, None, None, (1,), outs(last))
    near_wait(last)
    join(last)
    far_start(last)
    lax.fori_loop(pairs - 1 - LAG, pairs, lambda j, _: (finish(j), 0)[1], 0)
    lax.fori_loop(last - 1 - LAG - HAND, pairs, lambda j, _: (hand(j), 0)[1], 0)

    def drain(j):
        for x in near(j):
            x.wait_send()

        @pl.when(owner(j) != chip)
        def _():
            for x in far(j, chip, owner(j)):
                x.wait_send()
            forward(seq(j, 1), j).wait_send()

        @pl.when(owner(j) == chip)
        def _():
            for x in spreads(j, seq(j, 1)):
                x.wait_send()
    for j in range(pairs):
        drain(j)

    def arrive(j):
        forward(seq(j, 0), j).wait_recv()
    for j in range(pairs):
        arrive(j)


def solution(mesh):
    n = mesh.shape["sp"]

    def step(q, k, v):
        B, L, _, D = k.shape
        H = q.shape[1]
        rows = L * G
        pairs = B // 2
        chips = n // 2
        own = pairs // chips
        f32, bf16, vmem, dma = jnp.float32, jnp.bfloat16, pltpu.VMEM, pltpu.SemaphoreType.DMA
        return pl.pallas_call(
            kernel,
            out_shape=pltpu.VMEM(q.shape, q.dtype),
            in_specs=[pl.BlockSpec(memory_space=pl.ANY)] * 3,
            out_specs=pl.BlockSpec(memory_space=pltpu.VMEM),
            scratch_shapes=[
                vmem((SLOTS, rows, D), bf16), vmem((SLOTS, rows, D), bf16), vmem((B, H, D), bf16), vmem((B, 2 * H, 2 * D), bf16),
                vmem((H, W), f32), vmem((2, rows // (2 * W), 2 * H, W), f32), vmem((2, rows // (2 * W), 2 * H, W), bf16),
                vmem((2, H, 128), f32), vmem((2, H, 128), f32), vmem((2, H, 128), f32),
                dma((SLOTS,)), dma((SLOTS,)), dma,
                vmem((pairs, H, D), bf16), vmem((pairs, 8, 128), f32), vmem((pairs, H, D), bf16), vmem((pairs, 8, 128), f32),
                vmem((pairs, H, D), f32), vmem((pairs, 8, 128), f32),
                vmem((pairs, H, D), bf16), vmem((pairs, 8, 128), f32),
                vmem((own, chips, H, D), bf16), vmem((own, chips, 8, 128), f32),
                vmem((own, H, D), bf16),
                dma((2, pairs)), dma((2, pairs)), dma((2, pairs)), dma((2, own, chips)), dma((chips, pairs)), dma((B,)),
            ],
            compiler_params=pltpu.CompilerParams(vmem_limit_bytes=58 << 20, collective_id=0, has_side_effects=True),
            name="attend",
        )(q, k.reshape(B, rows, D), v.reshape(B, rows, D))

    return jax.shard_map(
        step,
        mesh=mesh,
        in_specs=(P("dp", None, None), P("dp", "sp", None, None), P("dp", "sp", None, None)),
        out_specs=P("dp", None, None),
        check_vma=False,
    )
```

time: 49.1 us -> 39 us (0.79)
  Pallas kernels: 47.2 us -> 38 us
  local copies, waits for them, and re-layouts: 1.82 us -> 0.77 us
    pallas_call x1, Pallas kernels: 47.2 us -> 38 us  [step(): pl.pallas_call(kernel, out_shape=pltpu.VMEM(q.shape, q.dtype), in_specs=[...]
    unnamed x1, local copies, waits for them, and re-layouts: 1.82 us -> 0.77 us
where the time goes in v2:
time: 39 us; the launch traced here: 38.8 us
  Pallas kernels  38 us (97%)
  local copies, waits for them, and re-layouts  0.77 us (2%)
    pallas_call x1, Pallas kernels, step(): pl.pallas_call(kernel, out_shape=pltpu.VMEM(q.shape, q.dtype), in_specs=[...  38 us

profile of v2, /device:TPU:0, one launch (start us, length us, event | category | flops | bytes accessed | tf_op | source)
XLA Modules:
  0.0 38.8 jit_solution(10625550579805141238)
XLA Ops:
  0.0 38.0 %attend.1 = bf16[32,56,128]{2,1,0:T(8,128)(2,1)S(1)} custom-call(bf16[32,56,128]{2,1,0:T(8,128)(2,1)} %q_ref.1, bf16[32,4096,128]{2,1,0:T(8,128)(2,1)} %bitcast.2, bf16[32,4096,128]{2,1,0:T(8,128)(2,1)} %bitcast.3), custom_call_target="tpu_custom_call" | custom-call | tf_op jit(solution)/shard_map/attend/pallas_call | solution.py:345
  38.0 0.8 %copy.5 = bf16[32,56,128]{2,1,0:T(8,128)(2,1)} copy(bf16[32,56,128]{2,1,0:T(8,128)(2,1)S(1)} %attend.1) | data formatting | bytes 917504

commit v3 on v2

--- a/solution.py
+++ b/solution.py
@@ -13,13 +13,14 @@
 AHEAD = 3
 LAG = 7
 HAND = 6
+LATE = 1
 G = 8
 W = 256
 
 
 def kernel(q_ref, k_ref, v_ref, o_ref, kbuf, vbuf, qbuf, qq, bias, sbuf, pbuf, hbuf, mbuf, tbuf, ksem, vsem, qsem,
            near_out, near_out_st, near_in, near_in_st, mine, mine_st, far_out, far_out_st, far_in, far_in_st, done,
-           near_send, near_recv, far_send, far_recv, all_send, all_recv):
+           near_send, near_recv, far_send, far_recv, all_send, all_recv, late_send):
     B, H, D = q_ref.shape
     S = H // G
     half = k_ref.shape[1] // 2
@@ -36,7 +37,7 @@
     def seq(j, u):
         return 2 * j + core if u else 2 * j + 1 - core
 
-    def owner(j):
+    def owner(j, core=core):
         low, high = (j >> 1) & 1, (j >> 2) & 1
         z = (2 * (1 ^ low) + (1 ^ low ^ high)) ^ (3 * core)
         return 4 * ((j ^ core) & 1) + z
@@ -66,6 +67,25 @@
             pltpu.make_async_remote_copy(far_out.at[j], far_in.at[s, at], far_send.at[0, j], far_recv.at[0, s, at], device_id=to, device_id_type=MESH),
             pltpu.make_async_remote_copy(far_out_st.at[j], far_in_st.at[s, at], far_send.at[1, j], far_recv.at[1, s, at], device_id=to, device_id_type=MESH),
         ]
+
+    first_late = pairs - LATE
+    late_place = far_in.shape[0] - LATE
+
+    def far_late(j, at, to):
+        s = late_place + j - first_late
+        to = {"sp": 2 * to + 1}
+        return [
+            pltpu.make_async_remote_copy(far_out.at[j], far_in.at[s, at], far_send.at[0, j], far_recv.at[0, s, at], device_id=to, device_id_type=MESH),
+            pltpu.make_async_remote_copy(far_out_st.at[j], far_in_st.at[s, at], far_send.at[1, j], far_recv.at[1, s, at], device_id=to, device_id_type=MESH),
+        ]
+
+    def spreads_late(j):
+        y, z = chip >> 2, chip & 3
+        to = [4 * ((y + dy) & 1) + ((z + dz) & 3) for dy, dz in ((1, 2), (0, 2), (1, 1), (1, 3), (0, 1), (0, 3), (1, 0))]
+        to = [2 * x + u for x in to for u in range(2)] + [2 * chip]
+        x = j - first_late
+        return [pltpu.make_async_remote_copy(done.at[late_place + x], o_ref.at[2 * j], late_send.at[x, i], all_recv.at[2 * j],
+                                             device_id={"sp": d}, device_id_type=MESH) for i, d in enumerate(to)]
 
     def spread(j, b, slot, chip_, core_):
         i = 2 * chip_ + core_
@@ -206,14 +226,39 @@
 
     def far_start(j):
         to = owner(j)
-
-        @pl.when(to != chip)
+        late = isinstance(j, int) and j >= first_late
+
+        @pl.when((to != chip) & ((core == 1) | (not late)))
         def _():
             for x in far(j, chip, to):
                 x.start()
+        if late:
+            @pl.when(core == 0)
+            def _():
+                for x in far_late(j, chip, owner(j, 0)):
+                    x.start()
+
+    def finish_late(j):
+        @pl.when((core == 1) & (owner(j, 0) == chip))
+        def _():
+            s = late_place + j - first_late
+            for x in range(chips):
+                for y in far_late(j, x, chip):
+                    y.wait_recv()
+            ws, _, total = merge([far_in_st[s, x] for x in range(chips)])
+            inverse = 1.0 / total
+            rows = None
+            for x, w in enumerate(ws):
+                new = scaled(far_in[s, x].astype(jnp.float32), w * inverse)
+                rows = new if rows is None else [y + z for y, z in zip(rows, new)]
+            out = jnp.concatenate(rows, 0).astype(jnp.bfloat16)
+            done[s] = out
+            o_ref[2 * j] = out
+            for x in spreads_late(j):
+                x.start()
 
     def finish(j):
-        @pl.when(owner(j) == chip)
+        @pl.when((owner(j) == chip) & ((core == 1) | (j < first_late)))
         def _():
             s = j >> 3
             b = seq(j, 1)
@@ -232,7 +277,7 @@
             o_ref[b] = done[s]
 
     def hand(j):
-        @pl.when(owner(j) != chip)
+        @pl.when((owner(j) != chip) & ((core == 1) | (j < first_late)))
         def _():
             b = seq(j, 1)
             forward(b, j).wait_recv()
@@ -306,29 +351,45 @@
     join(last)
     far_start(last)
     lax.fori_loop(pairs - 1 - LAG, pairs, lambda j, _: (finish(j), 0)[1], 0)
+    lax.fori_loop(first_late, pairs, lambda j, _: (finish_late(j), 0)[1], 0)
     lax.fori_loop(last - 1 - LAG - HAND, pairs, lambda j, _: (hand(j), 0)[1], 0)
 
-    def drain(j):
+    for j in range(pairs):
+        late = j >= first_late
         for x in near(j):
             x.wait_send()
 
-        @pl.when(owner(j) != chip)
+        @pl.when((owner(j) != chip) & ((core == 1) | (not late)))
         def _():
             for x in far(j, chip, owner(j)):
                 x.wait_send()
             forward(seq(j, 1), j).wait_send()
 
-        @pl.when(owner(j) == chip)
+        @pl.when((owner(j) == chip) & ((core == 1) | (not late)))
         def _():
             for x in spreads(j, seq(j, 1)):
                 x.wait_send()
+        if late:
+            @pl.when(core == 0)
+            def _():
+                for x in far_late(j, chip, owner(j, 0)):
+                    x.wait_send()
+
+            @pl.when((core == 1) & (owner(j, 0) == chip))
+            def _():
+                for x in spreads_late(j):
+                    x.wait_send()
     for j in range(pairs):
-        drain(j)
-
-    def arrive(j):
-        forward(seq(j, 0), j).wait_recv()
-    for j in range(pairs):
-        arrive(j)
+        if j < first_late:
+            forward(seq(j, 0), j).wait_recv()
+        else:
+            @pl.when((core == 0) | (owner(j, 0) != chip))
+            def _():
+                forward(2 * j, j).wait_recv()
+
+            @pl.when(core == 0)
+            def _():
+                forward(2 * j + 1, j).wait_recv()
 
 
 def solution(mesh):
@@ -355,9 +416,9 @@
                 vmem((pairs, H, D), bf16), vmem((pairs, 8, 128), f32), vmem((pairs, H, D), bf16), vmem((pairs, 8, 128), f32),
                 vmem((pairs, H, D), f32), vmem((pairs, 8, 128), f32),
                 vmem((pairs, H, D), bf16), vmem((pairs, 8, 128), f32),
-                vmem((own, chips, H, D), bf16), vmem((own, chips, 8, 128), f32),
-                vmem((own, H, D), bf16),
-                dma((2, pairs)), dma((2, pairs)), dma((2, pairs)), dma((2, own, chips)), dma((chips, pairs)), dma((B,)),
+                vmem((own + LATE, chips, H, D), bf16), vmem((own + LATE, chips, 8, 128), f32),
+                vmem((own + LATE, H, D), bf16),
+                dma((2, pairs)), dma((2, pairs)), dma((2, pairs)), dma((2, own + LATE, chips)), dma((chips, pairs)), dma((B,)), dma((LATE, n)),
             ],
             compiler_params=pltpu.CompilerParams(vmem_limit_bytes=58 << 20, collective_id=0, has_side_effects=True),
             name="attend",

time: 39 us -> 38.3 us (0.982)
  Pallas kernels: 38 us -> 37.3 us
    pallas_call x1, Pallas kernels: 38 us -> 37.3 us  [step(): pl.pallas_call(kernel, out_shape=pltpu.VMEM(q.shape, q.dtype), in_specs=[...]
where the time goes in v3:
time: 38.3 us; the launch traced here: 38.1 us
  Pallas kernels  37.3 us (97%)
  local copies, waits for them, and re-layouts  0.77 us (2%)
    pallas_call x1, Pallas kernels, step(): pl.pallas_call(kernel, out_shape=pltpu.VMEM(q.shape, q.dtype), in_specs=[...  37.3 us
    unnamed x1, local copies, waits for them, and re-layouts  0.77 us

profile of v3, /device:TPU:0, one launch (start us, length us, event | category | flops | bytes accessed | tf_op | source)
XLA Modules:
  0.0 38.1 jit_solution(5608830673754171532)
XLA Ops:
  0.0 37.3 %attend.1 = bf16[32,56,128]{2,1,0:T(8,128)(2,1)S(1)} custom-call(bf16[32,56,128]{2,1,0:T(8,128)(2,1)} %q_ref.1, bf16[32,4096,128]{2,1,0:T(8,128)(2,1)} %bitcast.2, bf16[32,4096,128]{2,1,0:T(8,128)(2,1)} %bitcast.3), custom_call_target="tpu_custom_call" | custom-call | tf_op jit(solution)/shard_map/attend/pallas_call | solution.py:406
  37.4 0.8 %copy.5 = bf16[32,56,128]{2,1,0:T(8,128)(2,1)} copy(bf16[32,56,128]{2,1,0:T(8,128)(2,1)S(1)} %attend.1) | data formatting | bytes 917504
